TPU v7x, 32 devices: a whole 2x2x4 slice. The times are simulated.
32 devices in a mesh: row: 8 (over z, x), col: 2 (over y), rep: 2 (over core).
Axes of the slice: x: 2, y: 2, z: 4, core: 2. Of those that a mesh axis runs over, the one named last changes fastest.
Arguments:
- matrix: float32 [16384, 16384], P('row', 'col'), may hold values from -0.125 to 0.125
- vectors: float32 [64, 16384], P('rep', 'row'), may hold values from -0.3 to 0.3
Outputs:
- result: float32 [64, 16384], P('rep', 'row')
All inputs are finite; a program needn't handle non-finite values.
Results may differ from a plain program's by a relative error of at most 0.00011.
Values sent between devices are 32-bit elements; how exact they have to be, the bound alone decides.
A program may use at most 128 MiB of HBM per device.

v0:
```python
import jax
import jax.numpy as jnp
from jax import lax
from jax.sharding import PartitionSpec as P

TERMS = 6
STEPS = 1


def broadcast(block, axis, holder):
    block = jnp.where(lax.axis_index(axis) == holder, block, jnp.zeros_like(block))
    return lax.psum(block, axis)


def apply_matrix(current, matrix):
    fanout = lax.axis_size("row") // lax.axis_size("col")
    column_index = lax.axis_index("col")
    pieces = [broadcast(current, "row", column_index * fanout + which) for which in range(fanout)]
    operand = jnp.concatenate(pieces, axis=1)
    partial_value = lax.dot_general(
        operand,
        matrix,
        (((1,), (1,)), ((), ())),
        precision=lax.Precision.HIGHEST,
        preferred_element_type=jnp.float32,
    )
    return lax.psum(partial_value, "col")


def local(matrix, vectors):
    summand = vectors
    running = vectors
    for degree in range(1, TERMS + 1):
        summand = apply_matrix(summand, matrix) / float(degree * STEPS)
        running = running + summand
    return running


def solution(mesh):
    placed = (P("row", "col"), P("rep", "row"))
    return jax.shard_map(
        local, mesh=mesh, in_specs=placed, out_specs=P("rep", "row"), check_vma=False
    )
```

profile of v0, /device:TPU:0, one launch (start us, length us, event | category | flops | bytes accessed | tf_op | source)
XLA Modules:
  0.0 1029.5 jit_solution(9411824174395434742)
XLA Ops:
  6.5 1.9 broadcast_select_fusion.7
  8.5 0.0 all-reduce.19.cloned.1.call-start
  8.6 83.8 %all-reduce.41.cloned.1.call-done = (f32[32,2048]{1,0:T(8,128)}, f32[32,2048]{1,0:T(8,128)}, f32[32,2048]{1,0:T(8,128)}, f32[32,2048]{1,0:T(8,128)}) async-done(((f32[32,2048]{1,0:T(8,128)}, f32[32,2048]{1,0:T(8,128)}, f32[32,2048]{1,0:T(8,128)}, f32[32,2048]{1,0:T(8,128)}), (f32[32,2048]{1,0:T(8,128)}, f32[32,2048]{1,0:T(8,128)}, f32[32,2048]{1,0:T(8,128)}, ...) | async-done | bytes 1048592 | tf_op jit(solution)/shard_map/psum | solution.py:12
  92.4 63.2 %fusion = f32[32,2048]{1,0:T(8,128)} fusion(f32[2048,8192]{1,0:T(8,128)} %param.2, f32[32,2048]{1,0:T(8,128)} %get-tuple-element.25, f32[32,2048]{1,0:T(8,128)} %get-tuple-element.26, f32[32,2048]{1,0:T(8,128)} %get-tuple-element.27, f32[32,2048]{1,0:T(8,128)} %get-tuple-element.28), kind=kOutput, calls=%fused_computation | convolution fusion | flops 6443237376 | bytes 68419584 | tf_op jit(solution)/shard_map/dot_general | solution.py:20
  155.6 0.0 all-reduce.39.cloned.1.call-start
  155.7 22.8 %all-reduce.19.cloned.1.call-done = f32[32,2048]{1,0:T(8,128)} async-done(((f32[32,2048]{1,0:T(8,128)}), f32[32,2048]{1,0:T(8,128)}) %all-reduce.19.cloned.1.call-update) | async-done | bytes 262160 | tf_op jit(solution)/shard_map/psum | solution.py:27
  178.5 1.9 broadcast_select_fusion.3
  180.4 0.3 all-reduce.21.cloned.1.call-start
  180.8 80.1 %all-reduce.39.cloned.1.call-done = (f32[32,2048]{1,0:T(8,128)}, f32[32,2048]{1,0:T(8,128)}, f32[32,2048]{1,0:T(8,128)}, f32[32,2048]{1,0:T(8,128)}) async-done(((f32[32,2048]{1,0:T(8,128)}, f32[32,2048]{1,0:T(8,128)}, f32[32,2048]{1,0:T(8,128)}, f32[32,2048]{1,0:T(8,128)}), (f32[32,2048]{1,0:T(8,128)}, f32[32,2048]{1,0:T(8,128)}, f32[32,2048]{1,0:T(8,128)}, ...) | async-done | bytes 1048592 | tf_op jit(solution)/shard_map/psum | solution.py:12
  260.8 63.2 %fusion.8 = f32[32,2048]{1,0:T(8,128)} fusion(f32[2048,8192]{1,0:T(8,128)} %param.2, f32[32,2048]{1,0:T(8,128)} %get-tuple-element.21, f32[32,2048]{1,0:T(8,128)} %get-tuple-element.22, f32[32,2048]{1,0:T(8,128)} %get-tuple-element.23, f32[32,2048]{1,0:T(8,128)} %get-tuple-element.24), kind=kOutput, calls=%fused_computation.8 | convolution fusion | flops 6443237376 | bytes 68419584 | tf_op jit(solution)/shard_map/dot_general | solution.py:20
  324.1 22.8 %all-reduce.21.cloned.1.call-done = f32[32,2048]{1,0:T(8,128)} async-done(((f32[32,2048]{1,0:T(8,128)}), f32[32,2048]{1,0:T(8,128)}) %all-reduce.21.cloned.1.call-update) | async-done | bytes 262160 | tf_op jit(solution)/shard_map/psum | solution.py:27
  347.0 1.9 multiply_select_fusion.15
  349.0 80.1 %all-reduce.37.cloned.1.call-done = (f32[32,2048]{1,0:T(8,128)}, f32[32,2048]{1,0:T(8,128)}, f32[32,2048]{1,0:T(8,128)}, f32[32,2048]{1,0:T(8,128)}) async-done(((f32[32,2048]{1,0:T(8,128)}, f32[32,2048]{1,0:T(8,128)}, f32[32,2048]{1,0:T(8,128)}, f32[32,2048]{1,0:T(8,128)}), (f32[32,2048]{1,0:T(8,128)}, f32[32,2048]{1,0:T(8,128)}, f32[32,2048]{1,0:T(8,128)}, ...) | async-done | bytes 1048592 | tf_op jit(solution)/shard_map/psum | solution.py:12
  429.1 63.2 %fusion.16 = f32[32,2048]{1,0:T(8,128)} fusion(f32[2048,8192]{1,0:T(8,128)} %param.2, f32[32,2048]{1,0:T(8,128)} %get-tuple-element.17, f32[32,2048]{1,0:T(8,128)} %get-tuple-element.18, f32[32,2048]{1,0:T(8,128)} %get-tuple-element.19, f32[32,2048]{1,0:T(8,128)} %get-tuple-element.20), kind=kOutput, calls=%fused_computation.16 | convolution fusion | flops 6443237376 | bytes 68419584 | tf_op jit(solution)/shard_map/dot_general | solution.py:20
  492.3 0.6 all-reduce.35.cloned.1.call-start
  492.9 22.3 %all-reduce.23.cloned.1.call-done = f32[32,2048]{1,0:T(8,128)} async-done(((f32[32,2048]{1,0:T(8,128)}), f32[32,2048]{1,0:T(8,128)}) %all-reduce.23.cloned.1.call-update) | async-done | bytes 262160 | tf_op jit(solution)/shard_map/psum | solution.py:27
  515.2 2.0 multiply_select_fusion.11
  517.2 0.0 all-reduce.25.cloned.1.call-start
  517.2 80.3 %all-reduce.35.cloned.1.call-done = (f32[32,2048]{1,0:T(8,128)}, f32[32,2048]{1,0:T(8,128)}, f32[32,2048]{1,0:T(8,128)}, f32[32,2048]{1,0:T(8,128)}) async-done(((f32[32,2048]{1,0:T(8,128)}, f32[32,2048]{1,0:T(8,128)}, f32[32,2048]{1,0:T(8,128)}, f32[32,2048]{1,0:T(8,128)}), (f32[32,2048]{1,0:T(8,128)}, f32[32,2048]{1,0:T(8,128)}, f32[32,2048]{1,0:T(8,128)}, ...) | async-done | bytes 1048592 | tf_op jit(solution)/shard_map/psum | solution.py:12
  597.5 63.2 %fusion.24 = f32[32,2048]{1,0:T(8,128)} fusion(f32[2048,8192]{1,0:T(8,128)} %param.2, f32[32,2048]{1,0:T(8,128)} %get-tuple-element.13, f32[32,2048]{1,0:T(8,128)} %get-tuple-element.14, f32[32,2048]{1,0:T(8,128)} %get-tuple-element.15, f32[32,2048]{1,0:T(8,128)} %get-tuple-element.16), kind=kOutput, calls=%fused_computation.24 | convolution fusion | flops 6443237376 | bytes 68419584 | tf_op jit(solution)/shard_map/dot_general | solution.py:20
  660.8 22.8 %all-reduce.25.cloned.1.call-done = f32[32,2048]{1,0:T(8,128)} async-done(((f32[32,2048]{1,0:T(8,128)}), f32[32,2048]{1,0:T(8,128)}) %all-reduce.25.cloned.1.call-update) | async-done | bytes 262160 | tf_op jit(solution)/shard_map/psum | solution.py:27
  683.6 2.0 multiply_select_fusion.7
  685.6 0.2 all-reduce.27.cloned.1.call-start
  685.8 80.2 %all-reduce.33.cloned.1.call-done = (f32[32,2048]{1,0:T(8,128)}, f32[32,2048]{1,0:T(8,128)}, f32[32,2048]{1,0:T(8,128)}, f32[32,2048]{1,0:T(8,128)}) async-done(((f32[32,2048]{1,0:T(8,128)}, f32[32,2048]{1,0:T(8,128)}, f32[32,2048]{1,0:T(8,128)}, f32[32,2048]{1,0:T(8,128)}), (f32[32,2048]{1,0:T(8,128)}, f32[32,2048]{1,0:T(8,128)}, f32[32,2048]{1,0:T(8,128)}, ...) | async-done | bytes 1048592 | tf_op jit(solution)/shard_map/psum | solution.py:12
  766.0 63.2 %fusion.32 = f32[32,2048]{1,0:T(8,128)} fusion(f32[2048,8192]{1,0:T(8,128)} %param.2, f32[32,2048]{1,0:T(8,128)} %get-tuple-element.9, f32[32,2048]{1,0:T(8,128)} %get-tuple-element.10, f32[32,2048]{1,0:T(8,128)} %get-tuple-element.11, f32[32,2048]{1,0:T(8,128)} %get-tuple-element.12), kind=kOutput, calls=%fused_computation.32 | convolution fusion | flops 6443237376 | bytes 68419584 | tf_op jit(solution)/shard_map/dot_general | solution.py:20
  829.3 22.8 %all-reduce.27.cloned.1.call-done = f32[32,2048]{1,0:T(8,128)} async-done(((f32[32,2048]{1,0:T(8,128)}), f32[32,2048]{1,0:T(8,128)}) %all-reduce.27.cloned.1.call-update) | async-done | bytes 262160 | tf_op jit(solution)/shard_map/psum | solution.py:27
  852.2 2.0 multiply_select_fusion.3
  854.2 0.3 all-reduce.29.cloned.1.call-start
  854.5 80.1 %all-reduce.31.cloned.1.call-done = (f32[32,2048]{1,0:T(8,128)}, f32[32,2048]{1,0:T(8,128)}, f32[32,2048]{1,0:T(8,128)}, f32[32,2048]{1,0:T(8,128)}) async-done(((f32[32,2048]{1,0:T(8,128)}, f32[32,2048]{1,0:T(8,128)}, f32[32,2048]{1,0:T(8,128)}, f32[32,2048]{1,0:T(8,128)}), (f32[32,2048]{1,0:T(8,128)}, f32[32,2048]{1,0:T(8,128)}, f32[32,2048]{1,0:T(8,128)}, ...) | async-done | bytes 1048592 | tf_op jit(solution)/shard_map/psum | solution.py:12
  934.5 63.2 %fusion.40 = f32[32,2048]{1,0:T(8,128)} fusion(f32[2048,8192]{1,0:T(8,128)} %param.2, f32[32,2048]{1,0:T(8,128)} %get-tuple-element.5, f32[32,2048]{1,0:T(8,128)} %get-tuple-element.6, f32[32,2048]{1,0:T(8,128)} %get-tuple-element.7, f32[32,2048]{1,0:T(8,128)} %get-tuple-element.8), kind=kOutput, calls=%fused_computation.40 | convolution fusion | flops 6443237376 | bytes 68419584 | tf_op jit(solution)/shard_map/dot_general | solution.py:20
  997.8 22.9 %all-reduce.29.cloned.1.call-done = f32[32,2048]{1,0:T(8,128)} async-done(((f32[32,2048]{1,0:T(8,128)}), f32[32,2048]{1,0:T(8,128)}) %all-reduce.29.cloned.1.call-update) | async-done | bytes 262160 | tf_op jit(solution)/shard_map/psum | solution.py:27
  1020.7 1.8 multiply_add_fusion
  (29 shorter events, 0.4 us)
Async XLA Ops:
  6.5 85.8 %all-reduce.41.cloned.1.call-start = ((), (), s32[]{:S(2)}) async-start(), calls=%async_computation.11 | async-start | bytes 2097152 | tf_op jit(solution)/shard_map/psum | solution.py:12
  8.5 170.0 %all-reduce.19.cloned.1.call-start = ((), (), s32[]{:S(2)}) async-start(), calls=%async_computation | async-start | bytes 524288 | tf_op jit(solution)/shard_map/psum | solution.py:27
  155.6 105.2 %all-reduce.39.cloned.1.call-start = ((), (), s32[]{:S(2)}) async-start(), calls=%async_computation.10 | async-start | bytes 2097152 | tf_op jit(solution)/shard_map/psum | solution.py:12
  180.4 166.5 %all-reduce.21.cloned.1.call-start = ((), (), s32[]{:S(2)}) async-start(), calls=%async_computation.1 | async-start | bytes 524288 | tf_op jit(solution)/shard_map/psum | solution.py:27
  324.1 105.0 %all-reduce.37.cloned.1.call-start = ((), (), s32[]{:S(2)}) async-start(), calls=%async_computation.9 | async-start | bytes 2097152 | tf_op jit(solution)/shard_map/psum | solution.py:12
  348.9 166.3 %all-reduce.23.cloned.1.call-start = ((), (), s32[]{:S(2)}) async-start(), calls=%async_computation.2 | async-start | bytes 524288 | tf_op jit(solution)/shard_map/psum | solution.py:27
  492.3 105.2 %all-reduce.35.cloned.1.call-start = ((), (), s32[]{:S(2)}) async-start(), calls=%async_computation.8 | async-start | bytes 2097152 | tf_op jit(solution)/shard_map/psum | solution.py:12
  517.2 166.5 %all-reduce.25.cloned.1.call-start = ((), (), s32[]{:S(2)}) async-start(), calls=%async_computation.3 | async-start | bytes 524288 | tf_op jit(solution)/shard_map/psum | solution.py:27
  660.8 105.2 %all-reduce.33.cloned.1.call-start = ((), (), s32[]{:S(2)}) async-start(), calls=%async_computation.7 | async-start | bytes 2097152 | tf_op jit(solution)/shard_map/psum | solution.py:12
  685.6 166.5 %all-reduce.27.cloned.1.call-start = ((), (), s32[]{:S(2)}) async-start(), calls=%async_computation.4 | async-start | bytes 524288 | tf_op jit(solution)/shard_map/psum | solution.py:27
  829.2 191.4 %copy-start = (f32[32,2048]{1,0:T(8,128)S(1)}, f32[32,2048]{1,0:T(8,128)}, u32[]{:S(2)}) copy-start(f32[32,2048]{1,0:T(8,128)} %param.3) | copy-start | bytes 786436
  829.2 191.4 %copy-start.1 = (f32[32,2048]{1,0:T(8,128)S(1)}, f32[32,2048]{1,0:T(8,128)}, u32[]{:S(2)}) copy-start(f32[32,2048]{1,0:T(8,128)} %all-reduce.19.cloned.1.call-done) | copy-start | bytes 786436
  829.2 191.4 %copy-start.2 = (f32[32,2048]{1,0:T(8,128)S(1)}, f32[32,2048]{1,0:T(8,128)}, u32[]{:S(2)}) copy-start(f32[32,2048]{1,0:T(8,128)} %all-reduce.21.cloned.1.call-done) | copy-start | bytes 786436
  829.2 191.4 %copy-start.3 = (f32[32,2048]{1,0:T(8,128)S(1)}, f32[32,2048]{1,0:T(8,128)}, u32[]{:S(2)}) copy-start(f32[32,2048]{1,0:T(8,128)} %all-reduce.23.cloned.1.call-done) | copy-start | bytes 786436
  829.2 191.4 %copy-start.4 = (f32[32,2048]{1,0:T(8,128)S(1)}, f32[32,2048]{1,0:T(8,128)}, u32[]{:S(2)}) copy-start(f32[32,2048]{1,0:T(8,128)} %all-reduce.25.cloned.1.call-done) | copy-start | bytes 786436
  829.3 105.2 %all-reduce.31.cloned.1.call-start = ((), (), s32[]{:S(2)}) async-start(), calls=%async_computation.6 | async-start | bytes 2097152 | tf_op jit(solution)/shard_map/psum | solution.py:12
  852.2 168.5 %copy-start.5 = (f32[32,2048]{1,0:T(8,128)S(1)}, f32[32,2048]{1,0:T(8,128)}, u32[]{:S(2)}) copy-start(f32[32,2048]{1,0:T(8,128)} %all-reduce.27.cloned.1.call-done) | copy-start | bytes 786436
  854.2 166.4 %all-reduce.29.cloned.1.call-start = ((), (), s32[]{:S(2)}) async-start(), calls=%async_computation.5 | async-start | bytes 524288 | tf_op jit(solution)/shard_map/psum | solution.py:27
Sparse Core Ops, SparseCore 0:
  11.2 81.1 all-reduce.40
  155.7 22.7 all-reduce.18
  182.3 78.4 all-reduce.38
  324.2 22.7 all-reduce.20
  350.7 78.3 all-reduce.36
  492.4 22.7 all-reduce.22
  519.0 78.4 all-reduce.34
  660.9 22.7 all-reduce.24
  687.5 78.4 all-reduce.32
  829.4 22.7 all-reduce.26
  856.0 78.4 all-reduce.30
  997.9 22.7 all-reduce.28
where the time goes:
time: 1030 us
  waiting for transfers between devices  621 us (60%)
  matrix products  379 us (37%)
  between operations  13.8 us (1%)
  other arithmetic  13.5 us (1%)
    psum x6, waiting for transfers between devices, broadcast(): return lax.psum(block, axis)  484 us
    dot_general x6, matrix products, apply_matrix(): lax.dot_general(operand, matrix, (((1,), (1,)), ((), ())), precision=lax....  379 us
    psum x6, waiting for transfers between devices, apply_matrix(): return lax.psum(partial_value, 'col')  136 us
  transfers between devices with their start and end apart: 12, of which 12 were waited for; matrix products, arithmetic and copies ran while one was open for 0% of the time, Pallas kernels for 0%

commit v1 on v0

--- a/solution.py
+++ b/solution.py
@@ -1,3 +1,4 @@
+import functools
 import jax
 import jax.numpy as jnp
 from jax import lax
@@ -5,6 +6,15 @@
 
 TERMS = 6
 STEPS = 1
+
+
+def create_the_loops(here_x, bus_axis):
+    shaped = lax.all_gather(here_x, bus_axis)
+    tall = jnp.sum(shaped, axis=0)
+    return tall
+
+
+modes_clear = functools.partial(create_the_loops, bus_axis="col")
 
 
 def broadcast(block, axis, holder):
@@ -24,7 +34,7 @@
         precision=lax.Precision.HIGHEST,
         preferred_element_type=jnp.float32,
     )
-    return lax.psum(partial_value, "col")
+    return modes_clear(partial_value)
 
 
 def local(matrix, vectors):

time: 1030 us -> 941 us (0.914)
  waiting for transfers between devices: 621 us -> 475 us
  blocking collectives: 0 us -> 48.3 us
  matrix products: 379 us -> 390 us
    psum x6 -> x0, waiting for transfers between devices: 136 us -> none  [apply_matrix(): return lax.psum(partial_value, 'col')]
    all_gather x0 -> x6, blocking collectives: none -> 48.3 us  [create_the_loops(): shaped = lax.all_gather(here_x, bus_axis)]
    dot_general x6, matrix products: 379 us -> 390 us  [apply_matrix(): lax.dot_general(operand, matrix, (((1,), (1,)), ((), ())), precision=lax....]
  transfers between devices with their start and end apart: 12 -> 6, of which waited for: 12 -> 6; matrix products, arithmetic and copies ran while one was open for 0% -> 0% of each run, Pallas kernels for 0% -> 0%
where the time goes in v1:
time: 941 us; the launch traced here: 936 us
  waiting for transfers between devices  475 us (50%)
  matrix products  390 us (41%)
  blocking collectives  48.3 us (5%)
  between operations  13.9 us (1%)
    psum x6, waiting for transfers between devices, broadcast(): return lax.psum(block, axis)  475 us
    dot_general x6, matrix products, apply_matrix(): lax.dot_general(operand, matrix, (((1,), (1,)), ((), ())), precision=lax....  390 us
    all_gather x6, blocking collectives, create_the_loops(): shaped = lax.all_gather(here_x, bus_axis)  48.3 us
  transfers between devices with their start and end apart: 6, of which 6 were waited for; matrix products, arithmetic and copies ran while one was open for 0% of the time, Pallas kernels for 0%

profile of v1, /device:TPU:0, one launch (start us, length us, event | category | flops | bytes accessed | tf_op | source)
XLA Modules:
  0.0 935.8 jit_solution(674097937612160043)
XLA Ops:
  6.5 1.9 broadcast_select_fusion.7
  8.5 0.0 all-reduce.23.cloned.1.call-update
  8.5 0.0 all-reduce.21.cloned.1.call-start
  8.5 83.8 %all-reduce.23.cloned.1.call-done = (f32[32,2048]{1,0:T(8,128)}, f32[32,2048]{1,0:T(8,128)}, f32[32,2048]{1,0:T(8,128)}, f32[32,2048]{1,0:T(8,128)}) async-done(((f32[32,2048]{1,0:T(8,128)}, f32[32,2048]{1,0:T(8,128)}, f32[32,2048]{1,0:T(8,128)}, f32[32,2048]{1,0:T(8,128)}), (f32[32,2048]{1,0:T(8,128)}, f32[32,2048]{1,0:T(8,128)}, f32[32,2048]{1,0:T(8,128)}, ...) | async-done | bytes 1048592 | tf_op jit(solution)/shard_map/psum | solution.py:22
  92.4 65.0 %fusion = f32[32,2048]{1,0:T(8,128)S(1)} fusion(f32[2048,8192]{1,0:T(8,128)} %param.2, f32[32,2048]{1,0:T(8,128)} %get-tuple-element.25, f32[32,2048]{1,0:T(8,128)} %get-tuple-element.26, f32[32,2048]{1,0:T(8,128)} %get-tuple-element.27, f32[32,2048]{1,0:T(8,128)} %get-tuple-element.28), kind=kOutput, calls=%fused_computation | convolution fusion | flops 6443237376 | bytes 68419584 | tf_op jit(solution)/shard_map/dot_general | solution.py:30
  157.4 8.0 all-gather
  165.4 1.0 broadcast_select_fusion.3
  166.4 0.0 all-reduce.21.cloned.1.call-update
  166.4 0.2 all-reduce.19.cloned.1.call-start
  166.7 78.1 %all-reduce.21.cloned.1.call-done = (f32[32,2048]{1,0:T(8,128)}, f32[32,2048]{1,0:T(8,128)}, f32[32,2048]{1,0:T(8,128)}, f32[32,2048]{1,0:T(8,128)}) async-done(((f32[32,2048]{1,0:T(8,128)}, f32[32,2048]{1,0:T(8,128)}, f32[32,2048]{1,0:T(8,128)}, f32[32,2048]{1,0:T(8,128)}), (f32[32,2048]{1,0:T(8,128)}, f32[32,2048]{1,0:T(8,128)}, f32[32,2048]{1,0:T(8,128)}, ...) | async-done | bytes 1048592 | tf_op jit(solution)/shard_map/psum | solution.py:22
  244.8 65.0 %fusion.8 = f32[32,2048]{1,0:T(8,128)S(1)} fusion(f32[2048,8192]{1,0:T(8,128)} %param.2, f32[32,2048]{1,0:T(8,128)} %get-tuple-element.21, f32[32,2048]{1,0:T(8,128)} %get-tuple-element.22, f32[32,2048]{1,0:T(8,128)} %get-tuple-element.23, f32[32,2048]{1,0:T(8,128)} %get-tuple-element.24), kind=kOutput, calls=%fused_computation.8 | convolution fusion | flops 6443237376 | bytes 68419584 | tf_op jit(solution)/shard_map/dot_general | solution.py:30
  309.8 8.0 all-gather.1
  317.8 1.0 multiply_select_fusion.15
  318.8 0.0 all-reduce.17.cloned.1.call-start
  318.9 78.2 %all-reduce.19.cloned.1.call-done = (f32[32,2048]{1,0:T(8,128)}, f32[32,2048]{1,0:T(8,128)}, f32[32,2048]{1,0:T(8,128)}, f32[32,2048]{1,0:T(8,128)}) async-done(((f32[32,2048]{1,0:T(8,128)}, f32[32,2048]{1,0:T(8,128)}, f32[32,2048]{1,0:T(8,128)}, f32[32,2048]{1,0:T(8,128)}), (f32[32,2048]{1,0:T(8,128)}, f32[32,2048]{1,0:T(8,128)}, f32[32,2048]{1,0:T(8,128)}, ...) | async-done | bytes 1048592 | tf_op jit(solution)/shard_map/psum | solution.py:22
  397.1 65.0 %fusion.16 = f32[32,2048]{1,0:T(8,128)S(1)} fusion(f32[2048,8192]{1,0:T(8,128)} %param.2, f32[32,2048]{1,0:T(8,128)} %get-tuple-element.17, f32[32,2048]{1,0:T(8,128)} %get-tuple-element.18, f32[32,2048]{1,0:T(8,128)} %get-tuple-element.19, f32[32,2048]{1,0:T(8,128)} %get-tuple-element.20), kind=kOutput, calls=%fused_computation.16 | convolution fusion | flops 6443237376 | bytes 68419584 | tf_op jit(solution)/shard_map/dot_general | solution.py:30
  462.2 8.2 all-gather.2
  470.4 1.0 multiply_select_fusion.11
  471.5 0.0 all-reduce.15.cloned.1.call-start
  471.5 78.3 %all-reduce.17.cloned.1.call-done = (f32[32,2048]{1,0:T(8,128)}, f32[32,2048]{1,0:T(8,128)}, f32[32,2048]{1,0:T(8,128)}, f32[32,2048]{1,0:T(8,128)}) async-done(((f32[32,2048]{1,0:T(8,128)}, f32[32,2048]{1,0:T(8,128)}, f32[32,2048]{1,0:T(8,128)}, f32[32,2048]{1,0:T(8,128)}), (f32[32,2048]{1,0:T(8,128)}, f32[32,2048]{1,0:T(8,128)}, f32[32,2048]{1,0:T(8,128)}, ...) | async-done | bytes 1048592 | tf_op jit(solution)/shard_map/psum | solution.py:22
  549.8 65.0 %fusion.24 = f32[32,2048]{1,0:T(8,128)S(1)} fusion(f32[2048,8192]{1,0:T(8,128)} %param.2, f32[32,2048]{1,0:T(8,128)} %get-tuple-element.13, f32[32,2048]{1,0:T(8,128)} %get-tuple-element.14, f32[32,2048]{1,0:T(8,128)} %get-tuple-element.15, f32[32,2048]{1,0:T(8,128)} %get-tuple-element.16), kind=kOutput, calls=%fused_computation.24 | convolution fusion | flops 6443237376 | bytes 68419584 | tf_op jit(solution)/shard_map/dot_general | solution.py:30
  614.8 8.0 all-gather.3
  622.8 1.0 multiply_select_fusion.7
  623.9 0.0 all-reduce.13.cloned.1.call-start
  623.9 78.2 %all-reduce.15.cloned.1.call-done = (f32[32,2048]{1,0:T(8,128)}, f32[32,2048]{1,0:T(8,128)}, f32[32,2048]{1,0:T(8,128)}, f32[32,2048]{1,0:T(8,128)}) async-done(((f32[32,2048]{1,0:T(8,128)}, f32[32,2048]{1,0:T(8,128)}, f32[32,2048]{1,0:T(8,128)}, f32[32,2048]{1,0:T(8,128)}), (f32[32,2048]{1,0:T(8,128)}, f32[32,2048]{1,0:T(8,128)}, f32[32,2048]{1,0:T(8,128)}, ...) | async-done | bytes 1048592 | tf_op jit(solution)/shard_map/psum | solution.py:22
  702.1 65.0 %fusion.32 = f32[32,2048]{1,0:T(8,128)S(1)} fusion(f32[2048,8192]{1,0:T(8,128)} %param.2, f32[32,2048]{1,0:T(8,128)} %get-tuple-element.9, f32[32,2048]{1,0:T(8,128)} %get-tuple-element.10, f32[32,2048]{1,0:T(8,128)} %get-tuple-element.11, f32[32,2048]{1,0:T(8,128)} %get-tuple-element.12), kind=kOutput, calls=%fused_computation.32 | convolution fusion | flops 6443237376 | bytes 68419584 | tf_op jit(solution)/shard_map/dot_general | solution.py:30
  767.2 8.1 all-gather.4
  775.4 1.0 multiply_select_fusion.3
  776.4 78.3 %all-reduce.13.cloned.1.call-done = (f32[32,2048]{1,0:T(8,128)}, f32[32,2048]{1,0:T(8,128)}, f32[32,2048]{1,0:T(8,128)}, f32[32,2048]{1,0:T(8,128)}) async-done(((f32[32,2048]{1,0:T(8,128)}, f32[32,2048]{1,0:T(8,128)}, f32[32,2048]{1,0:T(8,128)}, f32[32,2048]{1,0:T(8,128)}), (f32[32,2048]{1,0:T(8,128)}, f32[32,2048]{1,0:T(8,128)}, f32[32,2048]{1,0:T(8,128)}, ...) | async-done | bytes 1048592 | tf_op jit(solution)/shard_map/psum | solution.py:22
  854.7 65.0 %fusion.40 = f32[32,2048]{1,0:T(8,128)S(1)} fusion(f32[2048,8192]{1,0:T(8,128)} %param.2, f32[32,2048]{1,0:T(8,128)} %get-tuple-element.5, f32[32,2048]{1,0:T(8,128)} %get-tuple-element.6, f32[32,2048]{1,0:T(8,128)} %get-tuple-element.7, f32[32,2048]{1,0:T(8,128)} %get-tuple-element.8), kind=kOutput, calls=%fused_computation.40 | convolution fusion | flops 6443237376 | bytes 68419584 | tf_op jit(solution)/shard_map/dot_general | solution.py:30
  919.7 8.0 all-gather.5
  927.8 0.8 multiply_add_fusion
  (13 shorter events, 0.3 us)
Async XLA Ops:
  6.5 85.8 %all-reduce.23.cloned.1.call-start = ((), (), s32[]{:S(2)}) async-start(), calls=%async_computation.5 | async-start | bytes 2097152 | tf_op jit(solution)/shard_map/psum | solution.py:22
  8.5 236.3 %all-reduce.21.cloned.1.call-start = ((), (), s32[]{:S(2)}) async-start(), calls=%async_computation.4 | async-start | bytes 2097152 | tf_op jit(solution)/shard_map/psum | solution.py:22
  166.4 230.7 %all-reduce.19.cloned.1.call-start = ((), (), s32[]{:S(2)}) async-start(), calls=%async_computation.3 | async-start | bytes 2097152 | tf_op jit(solution)/shard_map/psum | solution.py:22
  318.8 230.9 %all-reduce.17.cloned.1.call-start = ((), (), s32[]{:S(2)}) async-start(), calls=%async_computation.2 | async-start | bytes 2097152 | tf_op jit(solution)/shard_map/psum | solution.py:22
  471.5 230.7 %all-reduce.15.cloned.1.call-start = ((), (), s32[]{:S(2)}) async-start(), calls=%async_computation.1 | async-start | bytes 2097152 | tf_op jit(solution)/shard_map/psum | solution.py:22
  623.9 230.8 %all-reduce.13.cloned.1.call-start = ((), (), s32[]{:S(2)}) async-start(), calls=%async_computation | async-start | bytes 2097152 | tf_op jit(solution)/shard_map/psum | solution.py:22
  767.2 160.6 %copy-start = (f32[32,2048]{1,0:T(8,128)S(1)}, f32[32,2048]{1,0:T(8,128)}, u32[]{:S(2)}) copy-start(f32[32,2048]{1,0:T(8,128)} %param.3) | copy-start | bytes 786436
Sparse Core Ops, SparseCore 0:
  11.2 81.1 all-reduce.22
  166.6 78.1 all-reduce.20
  319.0 78.1 all-reduce.18
  471.6 78.1 all-reduce.16
  624.0 78.1 all-reduce.14
  776.5 78.1 all-reduce.12
